TPU v7x, 32 devices: a whole 2x2x4 slice. The times are simulated.
32 devices in a mesh: dp: 8 (over z, y), tensor: 4 (over x, core).
Axes of the slice: x: 2, y: 2, z: 4, core: 2. Of those that a mesh axis runs over, the one named last changes fastest.
Arguments:
- patches: bfloat16 [8192, 1280], P('dp', 'tensor'), may hold values from -60 to 60
- counts: int32 [16], replicated, may hold values from 0 to 512, as said below
- first_gain: float32 [1280], replicated, may hold values from 0.1 to 1.9
- first_shift: float32 [1280], replicated, may hold values from -3 to 3
- in_weight: bfloat16 [1280, 3, 1280], P(None, None, 'tensor'), may hold values from -0.15625 to 0.15625
- in_bias: float32 [3, 1280], P(None, 'tensor'), may hold values from -30 to 30
- out_weight: bfloat16 [1280, 1280], P(None, 'tensor'), may hold values from -0.15625 to 0.15625
- out_bias: float32 [1280], P('tensor'), may hold values from -3 to 3
- second_gain: float32 [1280], P('tensor'), may hold values from 0.1 to 1.9
- second_shift: float32 [1280], P('tensor'), may hold values from -3 to 3
- merger_weight: bfloat16 [4, 1280, 4096], P(None, 'tensor', 'dp'), may hold values from -0.078125 to 0.078125
- merger_bias: float32 [4096], replicated, may hold values from -4 to 4
Outputs:
- embeds: bfloat16 [2048, 4096], P(('dp', 'tensor'))
Inputs may be any that keep to these rules, and one draw needn't show every extreme that they name: Entry 2 r + j is the patch count of slot j of data rank r, 0 for an empty slot; a rank's images fill its slots from slot 0; counts are multiples of 4; ranks 2 i and 2 i + 1 hold at most two images together, and in every draw some rank holds two.
All inputs are finite; a program needn't handle non-finite values.
Results may differ from a plain program's by a relative error of at most 0.0095.
Values may be sent and summed in bfloat16 or wider, within the bound.
No kernel may reach another device: no remote copies, remote signals or barrier semaphores. Data moves between devices by JAX's collectives and lax.ppermute only.
A program may use at most 128 MiB of HBM per device.

v0:
```python
import math
import jax
import jax.numpy as jnp
from jax import lax
from jax.sharding import PartitionSpec as P

D = 1280
HEADS = 16
LLMW = 4096
TILE = 512
SLOTS = 2
EPS = 1e-06
MASKED = -1e30


def from_partner(x, axis, stride):
    return lax.ppermute(x, axis, [(i, i ^ 1 << stride) for i in range(lax.axis_size(axis))])


def layer_norm(values, gain, shift):
    row_mean = jnp.mean(values, axis=-1, keepdims=True)
    centred = values - row_mean
    spread = jnp.mean(centred * centred, axis=-1, keepdims=True)
    return centred * lax.rsqrt(spread + EPS) * gain + shift


def encode(
    shard,
    slot_counts,
    first_gain,
    first_shift,
    in_weight,
    in_bias,
    out_weight,
    out_bias,
    second_gain,
    second_shift,
):
    number = slot_counts.shape[0]
    local_width = shard.shape[1]
    head_size = D // HEADS
    local_heads = local_width // head_size
    scale = 1.0 / math.sqrt(head_size)
    whole = lax.all_gather(shard, "tensor", axis=1, tiled=True)
    values = whole.astype(jnp.float32)
    normed = layer_norm(values, first_gain, first_shift).astype(jnp.bfloat16)
    projected = jnp.dot(
        normed, in_weight.reshape(D, 3 * local_width), preferred_element_type=jnp.float32
    )
    projected = (projected + in_bias.reshape(3 * local_width)).astype(jnp.bfloat16)
    projected = projected.reshape(number, TILE, 3, local_heads, head_size)
    queries = projected[:, :, 0]
    keys_tile = projected[:, :, 1]
    values_tile = projected[:, :, 2]
    scores = (
        jnp.einsum("nqhd,nkhd->nhqk", queries, keys_tile, preferred_element_type=jnp.float32)
        * scale
    )
    positions = jnp.arange(TILE, dtype=jnp.int32)
    key_live = positions[None, :] < slot_counts[:, None]
    scores = jnp.where(key_live[:, None, None, :], scores, MASKED)
    highest = jnp.max(scores, axis=-1, keepdims=True)
    raised = jnp.exp(scores - highest)
    weights = (raised / jnp.sum(raised, axis=-1, keepdims=True)).astype(jnp.bfloat16)
    heads_out = jnp.einsum(
        "nhqk,nkhd->nqhd", weights, values_tile, preferred_element_type=jnp.float32
    )
    heads_out = heads_out.astype(jnp.bfloat16).reshape(number * TILE, local_width)
    all_heads = lax.all_gather(heads_out, "tensor", axis=1, tiled=True)
    residual = (
        shard.astype(jnp.float32)
        + jnp.dot(all_heads, out_weight, preferred_element_type=jnp.float32)
        + out_bias
    )
    row_sum, row_squares = lax.psum(
        (jnp.sum(residual, axis=1), jnp.sum(residual * residual, axis=1)), "tensor"
    )
    row_mean = (row_sum / D)[:, None]
    second = (row_squares / D)[:, None]
    encoded = (residual - row_mean) * lax.rsqrt(
        second - row_mean * row_mean + EPS
    ) * second_gain + second_shift
    return encoded.astype(jnp.bfloat16).reshape(number * TILE // 4, 4 * local_width)


def rank_bit(rank, bit):
    return jnp.bitwise_and(jnp.right_shift(rank, bit), 1) == 1


def per_device(
    patches,
    counts,
    first_gain,
    first_shift,
    in_weight,
    in_bias,
    out_weight,
    out_bias,
    second_gain,
    second_shift,
    merger_weight,
    merger_bias,
):
    rank = lax.axis_index("dp")
    mine = lax.dynamic_slice_in_dim(counts, rank * SLOTS, SLOTS)
    weights_args = (
        first_gain,
        first_shift,
        in_weight,
        in_bias,
        out_weight,
        out_bias,
        second_gain,
        second_shift,
    )
    merged = encode(patches, mine, *weights_args)
    groups = lax.axis_size("tensor")
    quarter = SLOTS * TILE // 4 // groups
    ranks = lax.axis_size("dp")
    levels = ranks.bit_length() - 1
    rows_held = merged
    for bit in range(2):
        other = from_partner(rows_held, "dp", bit)
        rows_held = jnp.where(
            rank_bit(rank, bit),
            jnp.concatenate([other, rows_held], axis=0),
            jnp.concatenate([rows_held, other], axis=0),
        )
    column_held = merger_weight
    for bit in range(2, levels):
        other = from_partner(column_held, "dp", bit)
        column_held = jnp.where(
            rank_bit(rank, bit),
            jnp.concatenate([other, column_held], axis=2),
            jnp.concatenate([column_held, other], axis=2),
        )
    block_width = merger_weight.shape[2]
    column_total = column_held.shape[2]
    product = jnp.dot(
        rows_held, column_held.reshape(-1, column_total), preferred_element_type=jnp.float32
    )
    product = product.reshape(4, groups, quarter, column_total)
    summed = lax.psum_scatter(
        product.astype(jnp.bfloat16), "tensor", scatter_dimension=1, tiled=True
    ).astype(jnp.float32)
    within_quartet = jnp.bitwise_and(rank, 3)
    bias_columns = lax.dynamic_index_in_dim(
        merger_bias.reshape(ranks // 4, 4, block_width), within_quartet, 1, keepdims=False
    ).reshape(column_total)
    parcel = (summed + bias_columns).astype(jnp.bfloat16).reshape(2, 2, 1, quarter, column_total)
    for bit in range(2):
        owner_axis = 1 - bit
        high = rank_bit(rank, bit)
        lower_half = lax.index_in_dim(parcel, 0, owner_axis, keepdims=True)
        upper_half = lax.index_in_dim(parcel, 1, owner_axis, keepdims=True)
        kept = jnp.where(high, upper_half, lower_half)
        sent = jnp.where(high, lower_half, upper_half)
        other = from_partner(sent, "dp", bit)
        parcel = jnp.where(
            high, jnp.concatenate([other, kept], axis=2), jnp.concatenate([kept, other], axis=2)
        )
    parcel = parcel.reshape(4, quarter, ranks // 4, block_width)
    mixed = jnp.transpose(parcel, (1, 2, 0, 3)).reshape(quarter, LLMW)
    row_index = lax.axis_index("tensor") * quarter + jnp.arange(quarter, dtype=jnp.int32)
    slot_of_row = row_index // (TILE // 4)
    within = row_index % (TILE // 4)
    row_count = jnp.sum(
        jnp.where(
            slot_of_row[:, None] == jnp.arange(SLOTS, dtype=jnp.int32)[None, :], mine[None, :], 0
        ),
        axis=1,
    )
    keep = (within * 4 < row_count)[:, None]
    return jnp.where(keep, mixed, jnp.zeros_like(mixed))


def solution(mesh):
    return jax.shard_map(
        per_device,
        mesh=mesh,
        in_specs=(
            P("dp", "tensor"),
            P(),
            P(),
            P(),
            P(None, None, "tensor"),
            P(None, "tensor"),
            P(None, "tensor"),
            P("tensor"),
            P("tensor"),
            P("tensor"),
            P(None, "tensor", "dp"),
            P(),
        ),
        out_specs=P(("dp", "tensor"), None),
        check_vma=False,
    )
```

profile of v0, /device:TPU:0, one launch (start us, length us, event | category | flops | bytes accessed | tf_op | source)
XLA Modules:
  0.0 272.9 jit_solution(12721370287191470557)
XLA Ops:
  8.9 28.3 %all-gather.3.cloned.1.call-done = bf16[1024,1280]{0,1:T(8,128)(2,1)} async-done(((bf16[1024,320]{0,1:T(8,128)(2,1)}), bf16[1024,1280]{0,1:T(8,128)(2,1)}) %all-gather.3.cloned.1.call-update) | async-done | bytes 2621456 | tf_op jit(solution)/shard_map/all_gather | solution.py:44
  37.2 2.3 convert_reduce_fusion
  40.5 4.1 %add_convert_fusion = bf16[1024,960]{0,1:T(8,128)(2,1)} fusion(f32[960]{0:T(1024)S(1)} %add.107, bf16[1280,960]{0,1:T(8,128)(2,1)S(1)} %bitcast.68, bf16[1024,1280]{0,1:T(8,128)(2,1)S(1)} %copy-done.1, f32[1280]{0:T(1024)S(1)} %copy-done.6, f32[1280]{0:T(1024)S(1)} %copy-done.7, f32[1024]{0:T(1024)S(1)} %add_rsqrt_fusion.1, ...), kind=kOutput, calls=%fused_computation.17 | convolution fusion | flops 2526412800 | bytes 7067392 | tf_op jit(solution)/shard_map/dot_general | solution.py:47
  44.6 5.8 %reshape.191 = bf16[2,512,3,4,80]{1,0,4,3,2:T(2,128)(2,1)} reshape(bf16[1024,960]{0,1:T(8,128)(2,1)} %add_convert_fusion) | data formatting | bytes 3932160 | tf_op jit(solution)/shard_map/reshape | solution.py:51
  50.4 3.4 %fusion.46 = (bf16[2,512,1,4,80]{1,0,4,3,2:T(2,128)(2,1)S(1)}, bf16[2,512,1,4,80]{1,0,4,3,2:T(2,128)(2,1)}, bf16[2,512,1,4,80]{1,0,4,3,2:T(2,128)(2,1)}) fusion(bf16[2,512,3,4,80]{1,0,4,3,2:T(2,128)(2,1)} %reshape.191), kind=kLoop, calls=%fused_computation.75 | loop fusion | bytes 3932160 | tf_op jit(solution)/shard_map/slice | solution.py:54
  53.8 7.9 %fusion.47 = (f32[2,4,512]{2,1,0:T(4,128)S(1)}, f32[2,4,512,512]{2,3,1,0:T(8,128)}) fusion(pred[2,512]{1,0:T(4,128)(4,1)S(1)} %iota_compare_fusion, bf16[2,512,1,4,80]{1,0,4,3,2:T(2,128)(2,1)} %get-tuple-element.10, bf16[2,512,1,4,80]{1,0,4,3,2:T(2,128)(2,1)} %get-tuple-element.11), kind=kOutput, calls=%fused_computation.76 | convolution fusion | flops 343933440 | bytes 9716736 | tf_op jit(solution)/shard_map/sub | solution.py:63
  61.7 4.2 %fusion.34 = bf16[2,512,4,80]{1,3,2,0:T(8,128)(2,1)S(1)} fusion(f32[2,4,512,512]{2,3,1,0:T(8,128)} %get-tuple-element.19, f32[2,4,512]{2,1,0:T(4,128)S(1)} %get-tuple-element.18, bf16[2,512,1,4,80]{1,0,4,3,2:T(2,128)(2,1)S(1)} %get-tuple-element.9), kind=kOutput, calls=%fused_computation.40 | convolution fusion | flops 340066304 | bytes 9715712 | tf_op jit(solution)/shard_map/nhqk,nkhd->nqhd/dot_general | solution.py:65
  67.8 25.4 %all-gather.5.cloned.1.call-done = bf16[1024,1280]{0,1:T(8,128)(2,1)} async-done(((bf16[1024,320]{0,1:T(8,128)(2,1)}), bf16[1024,1280]{0,1:T(8,128)(2,1)}) %all-gather.5.cloned.1.call-update) | async-done | bytes 2621456 | tf_op jit(solution)/shard_map/all_gather | solution.py:69
  93.3 4.1 %fusion.45 = (f32[1024]{0:T(1024)S(1)}, f32[1024]{0:T(1024)S(1)}, f32[1024,320]{0,1:T(8,128)}) fusion(f32[320]{0:T(512)S(1)} %copy-done.8, bf16[1280,320]{0,1:T(8,128)(2,1)} %param.18, bf16[1024,1280]{0,1:T(8,128)(2,1)} %all-gather.5.cloned.1.call-done, bf16[1024,320]{0,1:T(8,128)(2,1)S(1)} %copy-done.2), kind=kOutput, calls=%fused_computation.74 | convolution fusion | flops 840824832 | bytes 5416192 | tf_op jit(solution)/shard_map/dot_general | solution.py:72
  97.4 6.0 %all-reduce.1 = (f32[1024]{0:T(1024)S(1)}, f32[1024]{0:T(1024)S(1)}) all-reduce(f32[1024]{0:T(1024)S(1)} %get-tuple-element.6, f32[1024]{0:T(1024)S(1)} %get-tuple-element.5), channel_id=1, replica_groups=mesh['dp'=8,'tensor'=4] {'tensor'}, use_global_device_ids=true, to_apply=%region_8.9 | all-reduce | flops 2048 | bytes 16384 | tf_op jit(solution)/shard_map/psum | solution.py:75
  103.4 2.4 add_convert_fusion.1
  107.3 1.6 reshape.193
  108.8 1.6 collective-permute-start
  110.5 14.8 %collective-permute-done = bf16[256,1280]{1,0:T(8,128)(2,1)S(1)} collective-permute-done((bf16[256,1280]{1,0:T(8,128)(2,1)}, bf16[256,1280]{1,0:T(8,128)(2,1)S(1)}, u32[]{:S(2)}, u32[]{:S(2)}) %collective-permute-start) | collective-permute-done | bytes 655392 | tf_op jit(solution)/shard_map/ppermute | solution.py:17
  125.3 2.7 maximum_select_fusion.2
  129.5 2.4 collective-permute-start.2
  131.9 53.7 %collective-permute-done.1 = bf16[512,1280]{1,0:T(8,128)(2,1)} collective-permute-done((bf16[512,1280]{1,0:T(8,128)(2,1)}, bf16[512,1280]{1,0:T(8,128)(2,1)}, u32[]{:S(2)}, u32[]{:S(2)}) %collective-permute-start.1) | collective-permute-done | bytes 1310752 | tf_op jit(solution)/shard_map/ppermute | solution.py:17
  185.6 2.8 %maximum_select_fusion = bf16[1024,1280]{1,0:T(8,128)(2,1)S(1)} fusion(bf16[512,1280]{1,0:T(8,128)(2,1)} %maximum_select_fusion.2, bf16[512,1280]{1,0:T(8,128)(2,1)} %collective-permute-done.1, pred[]{:T(512)S(6)} %eq.29), kind=kLoop, calls=%fused_computation.19 | loop fusion | flops 11796480 | bytes 5242881 | tf_op jit(solution)/shard_map/jit(_where)/select_n | solution.py:124
  188.5 7.0 %fusion.27 = bf16[4,4,64,1024]{3,2,1,0:T(8,128)(2,1)} fusion(bf16[4,4,64,1280]{3,2,1,0:T(8,128)(2,1)S(1)} %bitcast.71, bf16[1280,512]{1,0:T(8,128)(2,1)} %bitcast.7, bf16[1280,512]{1,0:T(8,128)(2,1)} %bitcast.6, pred[]{:T(512)S(6)} %eq.31), kind=kOutput, calls=%fused_computation.33 | convolution fusion | flops 2697199616 | bytes 7340033 | tf_op jit(solution)/shard_map/dot_general | solution.py:139
  196.1 49.8 %all-reduce.4.cloned.1.call-done = bf16[4,4,64,1024]{3,2,1,0:T(8,128)(2,1)} async-done(((bf16[4,4,64,1024]{3,2,1,0:T(8,128)(2,1)}), bf16[4,4,64,1024]{3,2,1,0:T(8,128)(2,1)}) %all-reduce.4.cloned.1.call-update) | async-done | bytes 2097168
  245.9 1.8 add_convert_fusion.2
  247.8 1.5 collective-permute-start.3
  249.3 6.3 %collective-permute-done.3 = bf16[2,1,1,64,1024]{4,3,1,0,2:T(8,128)(2,1)S(1)} collective-permute-done((bf16[2,1,1,64,1024]{4,3,1,0,2:T(8,128)(2,1)S(1)}, bf16[2,1,1,64,1024]{4,3,1,0,2:T(8,128)(2,1)S(1)}, u32[]{:S(2)}, u32[]{:S(2)}) %collective-permute-start.3) | collective-permute-done | bytes 262176 | tf_op jit(solution)/shard_map/ppermute | solution.py:17
  258.5 5.1 %collective-permute-done.4 = bf16[1,1,2,64,1024]{4,3,1,0,2:T(8,128)(2,1)S(1)} collective-permute-done((bf16[1,1,2,64,1024]{4,3,1,0,2:T(8,128)(2,1)}, bf16[1,1,2,64,1024]{4,3,1,0,2:T(8,128)(2,1)S(1)}, u32[]{:S(2)}, u32[]{:S(2)}) %collective-permute-start.4) | collective-permute-done | bytes 262176 | tf_op jit(solution)/shard_map/ppermute | solution.py:17
  (55 shorter events, 14.3 us)
Async XLA Ops:
  6.5 33.9 %copy-start = (bf16[1280,3,320]{0,2,1:T(8,128)(2,1)S(1)}, bf16[1280,3,320]{0,2,1:T(8,128)(2,1)}, u32[]{:S(2)}) copy-start(bf16[1280,3,320]{0,2,1:T(8,128)(2,1)} %param.16) | copy-start | bytes 7372804
  6.5 30.6 %all-gather.3.cloned.1.call-start = ((), (), s32[]{:S(2)}) async-start(), calls=%async_computation | async-start | bytes 3276800 | tf_op jit(solution)/shard_map/all_gather | solution.py:44
  7.3 86.0 %all-gather.5.cloned.1.call-start = ((), (), s32[]{:S(2)}) async-start(), calls=%async_computation.1 | async-start | bytes 3276800 | tf_op jit(solution)/shard_map/all_gather | solution.py:69
  8.9 31.6 %copy-start.6 = (f32[1280]{0:T(1024)S(1)}, f32[1280]{0:T(1024)}, u32[]{:S(2)}) copy-start(f32[1280]{0:T(1024)} %param.15) | copy-start | bytes 15364
  37.2 2.5 copy-start.1
  37.2 3.3 %copy-start.7 = (f32[1280]{0:T(1024)S(1)}, f32[1280]{0:T(1024)}, u32[]{:S(2)}) copy-start(f32[1280]{0:T(1024)} %param.14) | copy-start | bytes 15364
  65.9 27.4 %copy-start.2 = (bf16[1024,320]{0,1:T(8,128)(2,1)S(1)}, bf16[1024,320]{0,1:T(8,128)(2,1)}, u32[]{:S(2)}) copy-start(bf16[1024,320]{0,1:T(8,128)(2,1)} %param.12) | copy-start | bytes 1966084
  65.9 27.4 %copy-start.8 = (f32[320]{0:T(512)S(1)}, f32[320]{0:T(512)}, u32[]{:S(2)}) copy-start(f32[320]{0:T(512)} %param.19) | copy-start | bytes 3844
  67.6 35.8 %copy-start.4 = (f32[320]{0:T(512)S(1)}, f32[320]{0:T(512)}, u32[]{:S(2)}) copy-start(f32[320]{0:T(512)} %param.21) | copy-start | bytes 3844
  67.6 35.8 %copy-start.5 = (f32[320]{0:T(512)S(1)}, f32[320]{0:T(512)}, u32[]{:S(2)}) copy-start(f32[320]{0:T(512)} %param.20) | copy-start | bytes 3844
  67.6 178.3 %all-reduce.4.cloned.1.call-start = ((), (), s32[]{:S(2)}) async-start(), calls=%async_computation.2 | async-start | bytes 4194304
  108.8 16.4 %collective-permute-start = (bf16[256,1280]{1,0:T(8,128)(2,1)}, bf16[256,1280]{1,0:T(8,128)(2,1)S(1)}, u32[]{:S(2)}, u32[]{:S(2)}) collective-permute-start(bf16[256,1280]{1,0:T(8,128)(2,1)} %reshape.193), channel_id=1, source_target_pairs={{0,4},{4,0},{8,12},{12,8},{16,20},{20,16},{24,28},{28,24},{1,5},{5... | collective-permute-start | bytes 1966088 | tf_op jit(solution)/shard_map/ppermute | solution.py:17
  128.0 57.6 %collective-permute-start.1 = (bf16[512,1280]{1,0:T(8,128)(2,1)}, bf16[512,1280]{1,0:T(8,128)(2,1)}, u32[]{:S(2)}, u32[]{:S(2)}) collective-permute-start(bf16[512,1280]{1,0:T(8,128)(2,1)} %maximum_select_fusion.2), channel_id=1, source_target_pairs={{0,8},{4,12},{8,0},{12,4},{16,24},{20,28},{24,16},{28,20},{1,9},{5... | collective-permute-start | bytes 3932168 | tf_op jit(solution)/shard_map/ppermute | solution.py:17
  129.5 58.9 %collective-permute-start.2 = (bf16[4,320,512]{2,1,0:T(8,128)(2,1)}, bf16[4,320,512]{2,1,0:T(8,128)(2,1)}, u32[]{:S(2)}, u32[]{:S(2)}) collective-permute-start(bf16[4,320,512]{2,1,0:T(8,128)(2,1)} %param.22), channel_id=1, source_target_pairs={{0,16},{4,20},{8,24},{12,28},{16,0},{20,4},{24,8},{28,12},{1,17},{... | collective-permute-start | bytes 3932168 | tf_op jit(solution)/shard_map/ppermute | solution.py:17
  188.4 7.0 %copy-start.3 = (f32[4096]{0:T(1024)S(1)}, f32[4096]{0:T(1024)}, u32[]{:S(2)}) copy-start(f32[4096]{0:T(1024)} %param.23) | copy-start | bytes 49156
  188.5 7.1 %copy-start.9 = (u32[32]{0:T(128)S(1)}, u32[32]{0:T(128)}, u32[]{:S(2)}) copy-start(u32[32]{0:T(128)} %constant.74) | copy-start | bytes 388
  247.8 7.9 %collective-permute-start.3 = (bf16[2,1,1,64,1024]{4,3,1,0,2:T(8,128)(2,1)S(1)}, bf16[2,1,1,64,1024]{4,3,1,0,2:T(8,128)(2,1)S(1)}, u32[]{:S(2)}, u32[]{:S(2)}) collective-permute-start(bf16[2,1,1,64,1024]{4,3,1,0,2:T(8,128)(2,1)S(1)} %get-tuple-element.14), channel_id=1, source_target_pairs={{0,4},{4,0},{8,12},{12,8},{16,20},{20,16},{24,28},{28,24},{1,5},{5... | collective-permute-start | bytes 786440 | tf_op jit(solution)/shard_map/ppermute | solution.py:17
  256.5 7.2 %collective-permute-start.4 = (bf16[1,1,2,64,1024]{4,3,1,0,2:T(8,128)(2,1)}, bf16[1,1,2,64,1024]{4,3,1,0,2:T(8,128)(2,1)S(1)}, u32[]{:S(2)}, u32[]{:S(2)}) collective-permute-start(bf16[1,1,2,64,1024]{4,3,1,0,2:T(8,128)(2,1)} %get-tuple-element.12), channel_id=1, source_target_pairs={{0,8},{4,12},{8,0},{12,4},{16,24},{20,28},{24,16},{28,20},{1,9},{5... | collective-permute-start | bytes 786440 | tf_op jit(solution)/shard_map/ppermute | solution.py:17
Sparse Core Ops, SparseCore 0:
  8.9 28.2 all-gather.2
  67.7 25.5 all-gather.4
  195.6 50.2 all-reduce.3
where the time goes:
time: 273 us
  waiting for transfers between devices  184 us (67%)
  matrix products  27.4 us (10%)
  local copies, waits for them, and re-layouts  17.4 us (6%)
  other arithmetic  15.7 us (6%)
  between operations  13.4 us (5%)
  starting transfers between devices  8.81 us (3%)
  blocking collectives  5.97 us (2%)
    ppermute x5, waiting for transfers between devices, from_partner(): lax.ppermute(x, axis, [(i, i ^ 1 << stride) for i in range(lax.axis_size(...  80 us
    unnamed x4, waiting for transfers between devices  50.5 us
    all_gather x1, waiting for transfers between devices, encode(): whole = lax.all_gather(shard, 'tensor', axis=1, tiled=True)  28.3 us
    all_gather x1, waiting for transfers between devices, encode(): all_heads = lax.all_gather(heads_out, 'tensor', axis=1, tiled=True)  25.4 us
    ppermute x5, starting transfers between devices, from_partner(): lax.ppermute(x, axis, [(i, i ^ 1 << stride) for i in range(lax.axis_size(...  8.55 us
    sub x1, matrix products, encode(): raised = jnp.exp(scores - highest)  7.88 us
    dot_general x1, matrix products, per_device(): jnp.dot(rows_held, column_held.reshape(-1, column_total), preferred_eleme...  6.99 us
    psum x1, blocking collectives, encode(): lax.psum((jnp.sum(residual, axis=1), jnp.sum(residual * residual, axis=1)...  5.97 us
  transfers between devices with their start and end apart: 8, of which 7 were waited for; matrix products, arithmetic and copies ran while one was open for 2% of the time, Pallas kernels for 0%

commit v1 on v0

--- a/solution.py
+++ b/solution.py
@@ -41,7 +41,23 @@
     head_size = D // HEADS
     local_heads = local_width // head_size
     scale = 1.0 / math.sqrt(head_size)
-    whole = lax.all_gather(shard, "tensor", axis=1, tiled=True)
+
+    def follow_the_leaves(z_in):
+        axis_key = "tensor"
+        parts_n = lax.axis_size(axis_key)
+        panels = [z_in]
+        src_i = 0
+        while src_i < parts_n - 1:
+            panels.append(
+                lax.ppermute(panels[-1], axis_key, [(b, (b + 1) % parts_n) for b in range(parts_n)])
+            )
+            src_i = src_i + 1
+        passed = jnp.roll(
+            jnp.concatenate(panels[::-1], 1), (lax.axis_index(axis_key) + 1) * z_in.shape[1], 1
+        )
+        return passed
+
+    whole = follow_the_leaves(shard)
     values = whole.astype(jnp.float32)
     normed = layer_norm(values, first_gain, first_shift).astype(jnp.bfloat16)
     projected = jnp.dot(

time: 273 us -> 281 us (1.029)
  local copies, waits for them, and re-layouts: 17.4 us -> 22.8 us
  waiting for transfers between devices: 184 us -> 187 us
    ppermute x0 -> x3, waiting for transfers between devices: none -> 29.2 us  [follow_the_leaves(): lax.ppermute(panels[-1], axis_key, [(b, (b + 1) % parts_n) for b in range...]
    all_gather x1 -> x0, waiting for transfers between devices: 28.3 us -> none  [encode(): whole = lax.all_gather(shard, 'tensor', axis=1, tiled=True)]
    unnamed x22 -> x31, local copies, waits for them, and re-layouts: 1.76 us -> 7.08 us
    unnamed x4 -> x3, waiting for transfers between devices: 50.5 us -> 49.8 us
  transfers between devices with their start and end apart: 8 -> 10, of which waited for: 7 -> 9; matrix products, arithmetic and copies ran while one was open for 2% -> 2% of each run, Pallas kernels for 0% -> 0%
where the time goes in v1:
time: 281 us; the launch traced here: 280 us
  waiting for transfers between devices  187 us (67%)
  matrix products  27.6 us (10%)
  local copies, waits for them, and re-layouts  22.8 us (8%)
  other arithmetic  14.5 us (5%)
  between operations  13.7 us (5%)
  starting transfers between devices  9.1 us (3%)
  blocking collectives  5.97 us (2%)
    ppermute x5, waiting for transfers between devices, from_partner(): lax.ppermute(x, axis, [(i, i ^ 1 << stride) for i in range(lax.axis_size(...  80 us
    unnamed x3, waiting for transfers between devices  49.8 us
    ppermute x3, waiting for transfers between devices, follow_the_leaves(): lax.ppermute(panels[-1], axis_key, [(b, (b + 1) % parts_n) for b in range...  29.2 us
    all_gather x1, waiting for transfers between devices, encode(): all_heads = lax.all_gather(heads_out, 'tensor', axis=1, tiled=True)  27.6 us
    ppermute x5, starting transfers between devices, from_partner(): lax.ppermute(x, axis, [(i, i ^ 1 << stride) for i in range(lax.axis_size(...  8.55 us
    sub x1, matrix products, encode(): raised = jnp.exp(scores - highest)  7.9 us
    unnamed x31, local copies, waits for them, and re-layouts  7.08 us
    dot_general x1, matrix products, per_device(): jnp.dot(rows_held, column_held.reshape(-1, column_total), preferred_eleme...  6.96 us
  transfers between devices with their start and end apart: 10, of which 9 were waited for; matrix products, arithmetic and copies ran while one was open for 2% of the time, Pallas kernels for 0%

profile of v1, /device:TPU:0, one launch (start us, length us, event | category | flops | bytes accessed | tf_op | source)
XLA Modules:
  0.0 280.4 jit_solution(15891813722138344927)
XLA Ops:
  7.0 10.4 %collective-permute-done = bf16[1024,320]{0,1:T(8,128)(2,1)S(1)} collective-permute-done((bf16[1024,320]{0,1:T(8,128)(2,1)}, bf16[1024,320]{0,1:T(8,128)(2,1)S(1)}, u32[]{:S(2)}, u32[]{:S(2)}) %collective-permute-start) | collective-permute-done | bytes 655392 | tf_op jit(solution)/shard_map/ppermute | solution.py:52
  18.3 10.1 %collective-permute-done.1 = bf16[1024,320]{0,1:T(8,128)(2,1)} collective-permute-done((bf16[1024,320]{0,1:T(8,128)(2,1)S(1)}, bf16[1024,320]{0,1:T(8,128)(2,1)}, u32[]{:S(2)}, u32[]{:S(2)}) %collective-permute-start.1) | collective-permute-done | bytes 655392 | tf_op jit(solution)/shard_map/ppermute | solution.py:52
  30.1 8.7 %collective-permute-done.2 = bf16[1024,320]{0,1:T(8,128)(2,1)} collective-permute-done((bf16[1024,320]{0,1:T(8,128)(2,1)}, bf16[1024,320]{0,1:T(8,128)(2,1)}, u32[]{:S(2)}, u32[]{:S(2)}) %collective-permute-start.2) | collective-permute-done | bytes 655392 | tf_op jit(solution)/shard_map/ppermute | solution.py:52
  45.4 4.1 %add_convert_fusion = bf16[1024,960]{0,1:T(8,128)(2,1)} fusion(f32[960]{0:T(1024)S(1)} %add.123, bf16[1280,960]{0,1:T(8,128)(2,1)S(1)} %bitcast.68, f32[1280]{0:T(1024)S(1)} %copy-done.7, f32[1280]{0:T(1024)S(1)} %copy-done.8, f32[1024]{0:T(1024)S(1)} %add_rsqrt_fusion.1, f32[1024]{0:T(1024)S(1)} %broadcast_multiply_fusion.1, ...), kind=kOutput, calls=%fused_computation.17 | convolution fusion | flops 2526412800 | bytes 7073796 | tf_op jit(solution)/shard_map/dot_general | solution.py:63
  49.6 5.8 %reshape.191 = bf16[2,512,3,4,80]{1,0,4,3,2:T(2,128)(2,1)} reshape(bf16[1024,960]{0,1:T(8,128)(2,1)} %add_convert_fusion) | data formatting | bytes 3932160 | tf_op jit(solution)/shard_map/reshape | solution.py:67
  55.3 3.4 %fusion.48 = (bf16[2,512,1,4,80]{1,0,4,3,2:T(2,128)(2,1)}, bf16[2,512,1,4,80]{1,0,4,3,2:T(2,128)(2,1)}, bf16[2,512,1,4,80]{1,0,4,3,2:T(2,128)(2,1)}) fusion(bf16[2,512,3,4,80]{1,0,4,3,2:T(2,128)(2,1)} %reshape.191), kind=kLoop, calls=%fused_computation.85 | loop fusion | bytes 3932160 | tf_op jit(solution)/shard_map/slice | solution.py:70
  58.7 7.9 %fusion.49 = (f32[2,4,512]{2,1,0:T(4,128)S(1)}, f32[2,4,512,512]{2,3,1,0:T(8,128)}) fusion(pred[2,512]{1,0:T(4,128)(4,1)S(1)} %iota_compare_fusion, bf16[2,512,1,4,80]{1,0,4,3,2:T(2,128)(2,1)} %get-tuple-element.10, bf16[2,512,1,4,80]{1,0,4,3,2:T(2,128)(2,1)} %get-tuple-element.11), kind=kOutput, calls=%fused_computation.86 | convolution fusion | flops 343933440 | bytes 9716736 | tf_op jit(solution)/shard_map/sub | solution.py:79
  66.6 4.5 %fusion.35 = bf16[2,512,4,80]{1,3,2,0:T(8,128)(2,1)S(1)} fusion(f32[2,4,512,512]{2,3,1,0:T(8,128)} %get-tuple-element.19, f32[2,4,512]{2,1,0:T(4,128)S(1)} %get-tuple-element.18, bf16[2,512,1,4,80]{1,0,4,3,2:T(2,128)(2,1)} %get-tuple-element.9), kind=kOutput, calls=%fused_computation.41 | convolution fusion | flops 340066304 | bytes 9715712 | tf_op jit(solution)/shard_map/nhqk,nkhd->nqhd/dot_general | solution.py:81
  72.8 27.6 %all-gather.2.cloned.1.call-done = bf16[1024,1280]{0,1:T(8,128)(2,1)} async-done(((bf16[1024,320]{0,1:T(8,128)(2,1)}), bf16[1024,1280]{0,1:T(8,128)(2,1)}) %all-gather.2.cloned.1.call-update) | async-done | bytes 2621456 | tf_op jit(solution)/shard_map/all_gather | solution.py:85
  100.5 4.1 %fusion.47 = (f32[1024]{0:T(1024)S(1)}, f32[1024]{0:T(1024)S(1)}, f32[1024,320]{0,1:T(8,128)}) fusion(f32[320]{0:T(512)S(1)} %copy-done.9, bf16[1280,320]{0,1:T(8,128)(2,1)} %param.18, bf16[1024,1280]{0,1:T(8,128)(2,1)} %all-gather.2.cloned.1.call-done, bf16[1024,320]{0,1:T(8,128)(2,1)S(1)} %copy-done.1), kind=kOutput, calls=%fused_computation.84 | convolution fusion | flops 840824832 | bytes 5416192 | tf_op jit(solution)/shard_map/dot_general | solution.py:88
  104.6 6.0 %all-reduce.1 = (f32[1024]{0:T(1024)S(1)}, f32[1024]{0:T(1024)S(1)}) all-reduce(f32[1024]{0:T(1024)S(1)} %get-tuple-element.6, f32[1024]{0:T(1024)S(1)} %get-tuple-element.5), channel_id=1, replica_groups=mesh['dp'=8,'tensor'=4] {'tensor'}, use_global_device_ids=true, to_apply=%region_8.9 | all-reduce | flops 2048 | bytes 16384 | tf_op jit(solution)/shard_map/psum | solution.py:91
  110.6 2.4 add_convert_fusion.1
  114.4 1.6 reshape.193
  116.0 1.6 collective-permute-start.3
  117.7 14.8 %collective-permute-done.3 = bf16[256,1280]{1,0:T(8,128)(2,1)S(1)} collective-permute-done((bf16[256,1280]{1,0:T(8,128)(2,1)}, bf16[256,1280]{1,0:T(8,128)(2,1)S(1)}, u32[]{:S(2)}, u32[]{:S(2)}) %collective-permute-start.3) | collective-permute-done | bytes 655392 | tf_op jit(solution)/shard_map/ppermute | solution.py:17
  132.5 2.8 maximum_select_fusion.2
  136.7 2.4 collective-permute-start.5
  139.1 53.7 %collective-permute-done.4 = bf16[512,1280]{1,0:T(8,128)(2,1)} collective-permute-done((bf16[512,1280]{1,0:T(8,128)(2,1)}, bf16[512,1280]{1,0:T(8,128)(2,1)}, u32[]{:S(2)}, u32[]{:S(2)}) %collective-permute-start.4) | collective-permute-done | bytes 1310752 | tf_op jit(solution)/shard_map/ppermute | solution.py:17
  192.9 2.8 maximum_select_fusion
  195.7 7.0 %fusion.28 = bf16[4,4,64,1024]{3,2,1,0:T(8,128)(2,1)} fusion(bf16[4,4,64,1280]{3,2,1,0:T(8,128)(2,1)S(1)} %bitcast.71, bf16[1280,512]{1,0:T(8,128)(2,1)} %bitcast.7, bf16[1280,512]{1,0:T(8,128)(2,1)} %bitcast.6, pred[]{:T(512)S(6)} %eq.34), kind=kOutput, calls=%fused_computation.34 | convolution fusion | flops 2697199616 | bytes 7340033 | tf_op jit(solution)/shard_map/dot_general | solution.py:155
  203.3 49.8 %all-reduce.4.cloned.1.call-done = bf16[4,4,64,1024]{3,2,1,0:T(8,128)(2,1)} async-done(((bf16[4,4,64,1024]{3,2,1,0:T(8,128)(2,1)}), bf16[4,4,64,1024]{3,2,1,0:T(8,128)(2,1)}) %all-reduce.4.cloned.1.call-update) | async-done | bytes 2097168
  253.1 1.8 add_convert_fusion.2
  256.5 6.3 %collective-permute-done.6 = bf16[2,1,1,64,1024]{4,3,1,0,2:T(8,128)(2,1)S(1)} collective-permute-done((bf16[2,1,1,64,1024]{4,3,1,0,2:T(8,128)(2,1)S(1)}, bf16[2,1,1,64,1024]{4,3,1,0,2:T(8,128)(2,1)S(1)}, u32[]{:S(2)}, u32[]{:S(2)}) %collective-permute-start.6) | collective-permute-done | bytes 262176 | tf_op jit(solution)/shard_map/ppermute | solution.py:17
  265.7 5.1 %collective-permute-done.7 = bf16[1,1,2,64,1024]{4,3,1,0,2:T(8,128)(2,1)S(1)} collective-permute-done((bf16[1,1,2,64,1024]{4,3,1,0,2:T(8,128)(2,1)}, bf16[1,1,2,64,1024]{4,3,1,0,2:T(8,128)(2,1)S(1)}, u32[]{:S(2)}, u32[]{:S(2)}) %collective-permute-start.7) | collective-permute-done | bytes 262176 | tf_op jit(solution)/shard_map/ppermute | solution.py:17
  (68 shorter events, 22.0 us)
Async XLA Ops:
  6.5 38.9 %copy-start = (bf16[1280,3,320]{0,2,1:T(8,128)(2,1)S(1)}, bf16[1280,3,320]{0,2,1:T(8,128)(2,1)}, u32[]{:S(2)}) copy-start(bf16[1280,3,320]{0,2,1:T(8,128)(2,1)} %param.16) | copy-start | bytes 7372804
  6.5 34.5 %copy-start.1 = (bf16[1024,320]{0,1:T(8,128)(2,1)S(1)}, bf16[1024,320]{0,1:T(8,128)(2,1)}, u32[]{:S(2)}) copy-start(bf16[1024,320]{0,1:T(8,128)(2,1)} %param.12) | copy-start | bytes 1966084
  6.5 93.9 %all-gather.2.cloned.1.call-start = ((), (), s32[]{:S(2)}) async-start(), calls=%async_computation | async-start | bytes 3276800 | tf_op jit(solution)/shard_map/all_gather | solution.py:85
  6.5 10.9 %collective-permute-start = (bf16[1024,320]{0,1:T(8,128)(2,1)}, bf16[1024,320]{0,1:T(8,128)(2,1)S(1)}, u32[]{:S(2)}, u32[]{:S(2)}) collective-permute-start(bf16[1024,320]{0,1:T(8,128)(2,1)} %param.12), channel_id=1, source_target_pairs={{0,1},{1,2},{2,3},{3,0},{4,5},{5,6},{6,7},{7,4},{8,9},{9,10},{10,1... | collective-permute-start | bytes 1966088 | tf_op jit(solution)/shard_map/ppermute | solution.py:52
  17.5 0.8 copy-start.2
  18.3 10.1 %collective-permute-start.1 = (bf16[1024,320]{0,1:T(8,128)(2,1)S(1)}, bf16[1024,320]{0,1:T(8,128)(2,1)}, u32[]{:S(2)}, u32[]{:S(2)}) collective-permute-start(bf16[1024,320]{0,1:T(8,128)(2,1)S(1)} %collective-permute-done), channel_id=1, source_target_pairs={{0,1},{1,2},{2,3},{3,0},{4,5},{5,6},{6,7},{7,4},{8,9},{9,10},{10,1... | collective-permute-start | bytes 1966088 | tf_op jit(solution)/shard_map/ppermute | solution.py:52
  28.4 10.3 %collective-permute-start.2 = (bf16[1024,320]{0,1:T(8,128)(2,1)}, bf16[1024,320]{0,1:T(8,128)(2,1)}, u32[]{:S(2)}, u32[]{:S(2)}) collective-permute-start(bf16[1024,320]{0,1:T(8,128)(2,1)} %collective-permute-done.1), channel_id=1, source_target_pairs={{0,1},{1,2},{2,3},{3,0},{4,5},{5,6},{6,7},{7,4},{8,9},{9,10},{10,1... | collective-permute-start | bytes 1966088 | tf_op jit(solution)/shard_map/ppermute | solution.py:52
  29.2 11.8 %copy-start.3 = (bf16[1024,320]{0,1:T(8,128)(2,1)S(1)}, bf16[1024,320]{0,1:T(8,128)(2,1)}, u32[]{:S(2)}) copy-start(bf16[1024,320]{0,1:T(8,128)(2,1)} %copy-done.2) | copy-start | bytes 1966084
  43.5 1.9 copy-start.7
  43.5 1.9 copy-start.8
  71.1 29.4 %copy-start.9 = (f32[320]{0:T(512)S(1)}, f32[320]{0:T(512)}, u32[]{:S(2)}) copy-start(f32[320]{0:T(512)} %param.19) | copy-start | bytes 3844
  72.8 37.8 %copy-start.5 = (f32[320]{0:T(512)S(1)}, f32[320]{0:T(512)}, u32[]{:S(2)}) copy-start(f32[320]{0:T(512)} %param.21) | copy-start | bytes 3844
  72.8 37.8 %copy-start.6 = (f32[320]{0:T(512)S(1)}, f32[320]{0:T(512)}, u32[]{:S(2)}) copy-start(f32[320]{0:T(512)} %param.20) | copy-start | bytes 3844
  72.8 180.3 %all-reduce.4.cloned.1.call-start = ((), (), s32[]{:S(2)}) async-start(), calls=%async_computation.1 | async-start | bytes 4194304
  116.0 16.4 %collective-permute-start.3 = (bf16[256,1280]{1,0:T(8,128)(2,1)}, bf16[256,1280]{1,0:T(8,128)(2,1)S(1)}, u32[]{:S(2)}, u32[]{:S(2)}) collective-permute-start(bf16[256,1280]{1,0:T(8,128)(2,1)} %reshape.193), channel_id=1, source_target_pairs={{0,4},{4,0},{8,12},{12,8},{16,20},{20,16},{24,28},{28,24},{1,5},{5... | collective-permute-start | bytes 1966088 | tf_op jit(solution)/shard_map/ppermute | solution.py:17
  135.2 57.6 %collective-permute-start.4 = (bf16[512,1280]{1,0:T(8,128)(2,1)}, bf16[512,1280]{1,0:T(8,128)(2,1)}, u32[]{:S(2)}, u32[]{:S(2)}) collective-permute-start(bf16[512,1280]{1,0:T(8,128)(2,1)} %maximum_select_fusion.2), channel_id=1, source_target_pairs={{0,8},{4,12},{8,0},{12,4},{16,24},{20,28},{24,16},{28,20},{1,9},{5... | collective-permute-start | bytes 3932168 | tf_op jit(solution)/shard_map/ppermute | solution.py:17
  136.7 58.9 %collective-permute-start.5 = (bf16[4,320,512]{2,1,0:T(8,128)(2,1)}, bf16[4,320,512]{2,1,0:T(8,128)(2,1)}, u32[]{:S(2)}, u32[]{:S(2)}) collective-permute-start(bf16[4,320,512]{2,1,0:T(8,128)(2,1)} %param.22), channel_id=1, source_target_pairs={{0,16},{4,20},{8,24},{12,28},{16,0},{20,4},{24,8},{28,12},{1,17},{... | collective-permute-start | bytes 3932168 | tf_op jit(solution)/shard_map/ppermute | solution.py:17
  195.7 7.0 %copy-start.4 = (f32[4096]{0:T(1024)S(1)}, f32[4096]{0:T(1024)}, u32[]{:S(2)}) copy-start(f32[4096]{0:T(1024)} %param.23) | copy-start | bytes 49156
  195.7 7.0 %copy-start.10 = (u32[32]{0:T(128)S(1)}, u32[32]{0:T(128)}, u32[]{:S(2)}) copy-start(u32[32]{0:T(128)} %constant.94) | copy-start | bytes 388
  255.0 7.9 %collective-permute-start.6 = (bf16[2,1,1,64,1024]{4,3,1,0,2:T(8,128)(2,1)S(1)}, bf16[2,1,1,64,1024]{4,3,1,0,2:T(8,128)(2,1)S(1)}, u32[]{:S(2)}, u32[]{:S(2)}) collective-permute-start(bf16[2,1,1,64,1024]{4,3,1,0,2:T(8,128)(2,1)S(1)} %get-tuple-element.14), channel_id=1, source_target_pairs={{0,4},{4,0},{8,12},{12,8},{16,20},{20,16},{24,28},{28,24},{1,5},{5... | collective-permute-start | bytes 786440 | tf_op jit(solution)/shard_map/ppermute | solution.py:17
  263.7 7.2 %collective-permute-start.7 = (bf16[1,1,2,64,1024]{4,3,1,0,2:T(8,128)(2,1)}, bf16[1,1,2,64,1024]{4,3,1,0,2:T(8,128)(2,1)S(1)}, u32[]{:S(2)}, u32[]{:S(2)}) collective-permute-start(bf16[1,1,2,64,1024]{4,3,1,0,2:T(8,128)(2,1)} %get-tuple-element.12), channel_id=1, source_target_pairs={{0,8},{4,12},{8,0},{12,4},{16,24},{20,28},{24,16},{28,20},{1,9},{5... | collective-permute-start | bytes 786440 | tf_op jit(solution)/shard_map/ppermute | solution.py:17
Sparse Core Ops, SparseCore 0:
  72.9 27.5 all-gather.1
  202.8 50.2 all-reduce.3
